TPU v7x, 1024 devices: a whole 4x8x16 slice. The times are simulated.
1024 devices in a mesh: blk: 64 (over z, x), hub: 8 (over y), rep: 2 (over core).
Axes of the slice: x: 4, y: 8, z: 16, core: 2. Of those that a mesh axis runs over, the one named last changes fastest.
Arguments:
- source_feats: bfloat16 [262144, 512], P(('blk', 'hub', 'rep')), may hold values from -6 to 6
- target_feats: bfloat16 [524288, 512], P(('blk', 'hub', 'rep')), may hold values from -6 to 6
- hub_feats: bfloat16 [16384, 512], P(('blk', 'hub', 'rep')), may hold values from -6 to 6
- weight_self: bfloat16 [512, 256], replicated, may hold values from -0.25 to 0.25
- weight_neigh: bfloat16 [512, 256], replicated, may hold values from -0.25 to 0.25
- bias_vector: float32 [256], replicated, may hold values from -3 to 3
- send_rows: int32 [1024, 64, 32], P(('blk', 'hub', 'rep')), may hold values from 0 to 255
- edge_target: int32 [1024, 4096], P(('blk', 'hub', 'rep')), may hold values from 0 to 511
- edge_slot: int32 [1024, 4096], P(('blk', 'hub', 'rep')), may hold values from 0 to 2303, as said below
- hub_source: int32 [1024, 512], P(('blk', 'hub', 'rep')), may hold values from 0 to 255
- hub_target: int32 [1024, 512], P(('blk', 'hub', 'rep')), may hold values from 0 to 255
Outputs:
- vertex_out: bfloat16 [524288, 256], P(('blk', 'hub', 'rep'))
- hub_out: bfloat16 [16384, 256], P(('blk', 'hub', 'rep'))
Inputs may be any that keep to these rules, and one draw needn't show every extreme that they name: `edge_slot`: A value s < 2048 names slot s of table_d (row s % 32 of the block that blk index s // 32 sends); larger values name hubs of the device's blk index. For each device and blk index the slots named lie within a prefix of that block, of uneven length.
All inputs are finite; a program needn't handle non-finite values.
Results may differ from a plain program's by a relative error of at most 0.0025.
Values may be sent and summed in bfloat16 or wider, within the bound.
A program may use at most 32 MiB of HBM per device.

v0:
```python
import jax
import jax.numpy as jnp
from jax import lax
from jax.sharding import PartitionSpec as P


def in_blocks(array, dim, size):
    before, after = (array.shape[:dim], array.shape[dim + 1 :])
    return jnp.moveaxis(array.reshape(*before, size, -1, *after), dim, 0)


def sent_and_summed(array, axis, dim):
    size = lax.axis_size(axis)
    pieces = lax.all_to_all(in_blocks(array, dim, size), axis, 0, 0, tiled=True)
    return jnp.sum(pieces, axis=0)


def side_by_side(arrays, axis, dim, along):
    columns = [a.reshape(*a.shape[:along], -1) for a in arrays]
    both = jnp.concatenate(columns, axis=along)
    out, at, outs = (sent_and_summed(both, axis, dim), 0, [])
    for a, column in zip(arrays, columns):
        share = out[..., at : at + column.shape[along]]
        outs.append(share.reshape(*share.shape[:along], *a.shape[along:]))
        at += column.shape[along]
    return tuple(outs)


def on_device(
    source_feats,
    target_feats,
    hub_feats,
    weight_self,
    weight_neigh,
    bias_vector,
    send_rows,
    edge_target,
    edge_slot,
    hub_source,
    hub_target,
):
    width = weight_neigh.shape[1]
    local_proj = jnp.dot(source_feats, weight_neigh, preferred_element_type=jnp.float32).astype(
        jnp.bfloat16
    )
    picked = send_rows[0]
    outgoing = local_proj[picked]
    arrived = lax.all_to_all(outgoing, "blk", split_axis=0, concat_axis=0, tiled=True)
    hub_local = jnp.dot(hub_feats, weight_neigh, preferred_element_type=jnp.float32).astype(
        jnp.bfloat16
    )
    hub_table = lax.all_gather(hub_local, ("hub", "rep"), axis=0, tiled=True)
    group_hubs = lax.axis_size(("hub", "rep")) * hub_feats.shape[0]
    hub_source_rows = local_proj[hub_source[0]]
    hub_select = (
        hub_target[0][None, :] == jnp.arange(group_hubs, dtype=jnp.int32)[:, None]
    ).astype(jnp.bfloat16)
    hub_partial = jnp.dot(hub_select, hub_source_rows, preferred_element_type=jnp.float32)
    hub_edges = jnp.sum(hub_select.astype(jnp.float32), axis=1)
    hub_sum, hub_degree = side_by_side((hub_partial, hub_edges), ("hub", "rep"), 0, 1)
    table = jnp.concatenate([arrived.reshape(-1, width), hub_table], axis=0)
    gathered = table[edge_slot[0]]
    targets = target_feats.shape[0]
    select = (edge_target[0][None, :] == jnp.arange(targets, dtype=jnp.int32)[:, None]).astype(
        jnp.bfloat16
    )
    neigh_sum = jnp.dot(select, gathered, preferred_element_type=jnp.float32)
    degree = jnp.sum(select.astype(jnp.float32), axis=1)
    own = jnp.dot(target_feats, weight_self, preferred_element_type=jnp.float32)
    vertex_out = jnp.maximum(
        own + neigh_sum / jnp.maximum(degree, 1.0)[:, None] + bias_vector[None, :], 0.0
    ).astype(jnp.bfloat16)
    own_hub = jnp.dot(hub_feats, weight_self, preferred_element_type=jnp.float32)
    hub_out = jnp.maximum(
        own_hub + hub_sum / jnp.maximum(hub_degree, 1.0)[:, None] + bias_vector[None, :], 0.0
    ).astype(jnp.bfloat16)
    return (vertex_out, hub_out)


def solution(mesh):
    in_specs = (
        P(("blk", "hub", "rep"), None),
        P(("blk", "hub", "rep"), None),
        P(("blk", "hub", "rep"), None),
        P(),
        P(),
        P(),
        P(("blk", "hub", "rep"), None, None),
        P(("blk", "hub", "rep"), None),
        P(("blk", "hub", "rep"), None),
        P(("blk", "hub", "rep"), None),
        P(("blk", "hub", "rep"), None),
    )
    out_specs = (P(("blk", "hub", "rep"), None), P(("blk", "hub", "rep"), None))
    return jax.shard_map(
        on_device, mesh=mesh, in_specs=in_specs, out_specs=out_specs, check_vma=False
    )
```

profile of v0, /device:TPU:1, one launch (start us, length us, event | category | flops | bytes accessed | tf_op | source)
XLA Modules:
  0.0 128.3 jit_solution(11478420960607646475)
XLA Ops:
  0.6 0.0 copy-start
  0.6 0.0 copy-start.6
  0.7 0.7 compare_select_fusion.2
  1.4 0.8 convert_reduce_fusion.1
  2.2 1.3 convolution_convert_fusion
  3.5 0.0 copy-start.4
  3.5 2.0 %gather_fusion.2 = bf16[512,256]{1,0:T(8,128)(2,1)S(1)} fusion(bf16[256,256]{1,0:T(8,128)(2,1)S(1)} %convolution_convert_fusion, s32[1024]{0:T(1024)S(1)} %pad_clamp_fusion), kind=kCustom, calls=%fused_computation.2 | custom fusion | bytes 526336 | tf_op jit(solution)/shard_map/gather | solution.py:54
  5.5 0.0 copy-done.6
  5.5 0.2 fusion.11
  5.7 0.2 concatenate.15
  5.9 0.8 pad_maximum_fusion.1
  6.7 17.5 %all-to-all-start.1 = ((f32[16,16,257]{2,1,0:T(8,128)}), f32[16,16,257]{2,1,0:T(8,128)S(1)}, u32[]{:S(2)}, u32[]{:S(2)}) async-start(f32[16,16,257]{2,1,0:T(8,128)} %pad_maximum_fusion.1), calls=%async_computation.1 | async-start | bytes 786432 | tf_op jit(solution)/shard_map/all_to_all | solution.py:14
  24.2 0.0 copy-done.4
  24.2 0.1 copy.15
  24.3 0.1 reshape.104
  24.4 9.0 %gather_fusion = bf16[2048,256]{1,0:T(8,128)(2,1)} fusion(bf16[256,256]{1,0:T(8,128)(2,1)S(1)} %convolution_convert_fusion, s32[2048]{0:T(1024)S(1)} %broadcast_clamp_fusion.1), kind=kCustom, calls=%fused_computation | custom fusion | bytes 2105344 | tf_op jit(solution)/shard_map/gather | solution.py:47
  33.3 0.0 copy-start.1
  33.3 0.0 copy-start.3
  33.3 0.0 copy-start.8
  33.3 0.0 copy-start.5
  33.3 0.0 copy-start.2
  33.4 0.0 copy-start.7
  33.4 5.3 %all-to-all-done.1 = f32[16,16,257]{2,1,0:T(8,128)S(1)} async-done(((f32[16,16,257]{2,1,0:T(8,128)}), f32[16,16,257]{2,1,0:T(8,128)S(1)}, u32[]{:S(2)}, u32[]{:S(2)}) %all-to-all-start.1) | async-done | bytes 263200 | tf_op jit(solution)/shard_map/all_to_all | solution.py:14
  38.7 13.1 %all-to-all-start = ((bf16[64,32,256]{2,1,0:T(8,128)(2,1)}), bf16[64,32,256]{2,1,0:T(8,128)(2,1)S(1)}, u32[]{:S(2)}, u32[]{:S(2)}) async-start(bf16[64,32,256]{2,1,0:T(8,128)(2,1)} %bitcast.2), calls=%async_computation | async-start | bytes 2097152 | tf_op jit(solution)/shard_map/all_to_all | solution.py:48
  51.8 0.0 copy-done.1
  51.8 0.0 copy-done.3
  51.8 0.1 convolution_convert_fusion.1
  51.9 14.8 %all_gather.3 = bf16[256,256]{1,0:T(8,128)(2,1)S(1)} all-gather(bf16[16,256]{1,0:T(8,128)(2,1)S(1)} %convolution_convert_fusion.1), channel_id=1, replica_groups=mesh['blk'=64,'hub'=8,'rep'=2] {'hub','rep'}, dimensions={0}, use_global_device_ids=true | all-gather | bytes 139264 | tf_op jit(solution)/shard_map/all_gather | solution.py:52
  66.7 0.0 copy-done.8
  66.8 0.9 convert_reduce_fusion
  67.7 0.0 copy-done.5
  67.8 0.1 fusion.13
  67.9 0.0 copy-done.2
  67.9 0.0 copy-done.7
  67.9 0.8 fusion.9
  68.6 38.7 %all-to-all-done = bf16[64,32,256]{2,1,0:T(8,128)(2,1)S(1)} async-done(((bf16[64,32,256]{2,1,0:T(8,128)(2,1)}), bf16[64,32,256]{2,1,0:T(8,128)(2,1)S(1)}, u32[]{:S(2)}, u32[]{:S(2)}) %all-to-all-start) | async-done | bytes 1048608 | tf_op jit(solution)/shard_map/all_to_all | solution.py:48
  107.3 0.1 pad_maximum_fusion
  107.4 16.9 %gather_fusion.1 = bf16[4096,256]{1,0:T(8,128)(2,1)} fusion(bf16[2304,256]{1,0:T(8,128)(2,1)S(1)} %pad_maximum_fusion, s32[4096]{0:T(1024)S(1)} %broadcast_clamp_fusion), kind=kCustom, calls=%fused_computation.1 | custom fusion | bytes 4210688 | tf_op jit(solution)/shard_map/gather | solution.py:62
  124.3 3.0 %fusion.6 = f32[512,256]{1,0:T(8,128)S(1)} fusion(bf16[4096,256]{1,0:T(8,128)(2,1)} %gather_fusion.1, s32[4096]{0:T(1024)S(1)} %bitcast.32, f32[512]{0:T(512)S(1)} %broadcast_maximum_fusion), kind=kOutput, calls=%fused_computation.13 | convolution fusion | flops 1075970048 | bytes 2639872 | tf_op jit(solution)/shard_map/dot_general | solution.py:67
  127.3 0.0 copy-done
  127.3 1.0 fusion.5
  (7 shorter events, 0.1 us)
Async XLA Ops:
  0.6 126.7 %copy-start = (bf16[512,512]{1,0:T(8,128)(2,1)S(1)}, bf16[512,512]{1,0:T(8,128)(2,1)}, u32[]{:S(2)}) copy-start(bf16[512,512]{1,0:T(8,128)(2,1)} %param.12) | copy-start | bytes 1572868
  0.6 4.8 %copy-start.6 = (s32[1,512]{1,0:T(1,128)S(1)}, s32[1,512]{1,0:T(1,128)}, u32[]{:S(2)}) copy-start(s32[1,512]{1,0:T(1,128)} %param.21) | copy-start | bytes 6148
  3.5 20.7 %copy-start.4 = (s32[1,64,32]{1,2,0:T(8,128)S(1)}, s32[1,64,32]{1,2,0:T(8,128)}, u32[]{:S(2)}) copy-start(s32[1,64,32]{1,2,0:T(8,128)} %param.17) | copy-start | bytes 24580
  6.7 32.0 %all-to-all-start.1 = ((f32[16,16,257]{2,1,0:T(8,128)}), f32[16,16,257]{2,1,0:T(8,128)S(1)}, u32[]{:S(2)}, u32[]{:S(2)}) async-start(f32[16,16,257]{2,1,0:T(8,128)} %pad_maximum_fusion.1), calls=%async_computation.1 | async-start | bytes 786432 | tf_op jit(solution)/shard_map/all_to_all | solution.py:14
  33.3 18.4 %copy-start.1 = (bf16[512,256]{1,0:T(8,128)(2,1)S(1)}, bf16[512,256]{1,0:T(8,128)(2,1)}, u32[]{:S(2)}) copy-start(bf16[512,256]{1,0:T(8,128)(2,1)} %param.15) | copy-start | bytes 786436
  33.3 18.5 %copy-start.3 = (bf16[16,512]{1,0:T(8,128)(2,1)S(1)}, bf16[16,512]{1,0:T(8,128)(2,1)}, u32[]{:S(2)}) copy-start(bf16[16,512]{1,0:T(8,128)(2,1)} %param.13) | copy-start | bytes 49156
  33.3 33.4 %copy-start.8 = (s32[1,4096]{1,0:T(1,128)S(1)}, s32[1,4096]{1,0:T(1,128)}, u32[]{:S(2)}) copy-start(s32[1,4096]{1,0:T(1,128)} %param.18) | copy-start | bytes 49156
  33.3 34.3 %copy-start.5 = (s32[1,4096]{1,0:T(1,128)S(1)}, s32[1,4096]{1,0:T(1,128)}, u32[]{:S(2)}) copy-start(s32[1,4096]{1,0:T(1,128)} %param.19) | copy-start | bytes 49156
  33.3 34.5 %copy-start.2 = (bf16[512,256]{1,0:T(8,128)(2,1)S(1)}, bf16[512,256]{1,0:T(8,128)(2,1)}, u32[]{:S(2)}) copy-start(bf16[512,256]{1,0:T(8,128)(2,1)} %param.14) | copy-start | bytes 786436
  33.4 34.5 %copy-start.7 = (f32[256]{0:T(256)S(1)}, f32[256]{0:T(256)}, u32[]{:S(2)}) copy-start(f32[256]{0:T(256)} %param.16) | copy-start | bytes 3076
  38.7 68.6 %all-to-all-start = ((bf16[64,32,256]{2,1,0:T(8,128)(2,1)}), bf16[64,32,256]{2,1,0:T(8,128)(2,1)S(1)}, u32[]{:S(2)}, u32[]{:S(2)}) async-start(bf16[64,32,256]{2,1,0:T(8,128)(2,1)} %bitcast.2), calls=%async_computation | async-start | bytes 2097152 | tf_op jit(solution)/shard_map/all_to_all | solution.py:48
where the time goes:
time: 129 us; the launch traced here: 128 us
  waiting for transfers between devices  44 us (34%)
  starting transfers between devices  30.5 us (24%)
  local copies, waits for them, and re-layouts  28.3 us (22%)
  blocking collectives  14.8 us (11%)
  matrix products  6.36 us (5%)
  other arithmetic  3.54 us (3%)
    all_to_all x1, waiting for transfers between devices, on_device(): lax.all_to_all(outgoing, 'blk', split_axis=0, concat_axis=0, tiled=True)  38.7 us
    all_to_all x1, starting transfers between devices, sent_and_summed(): pieces = lax.all_to_all(in_blocks(array, dim, size), axis, 0, 0, tiled=True)  17.5 us
    gather x1, local copies, waits for them, and re-layouts, on_device(): gathered = table[edge_slot[0]]  16.9 us
    all_gather x1, blocking collectives, on_device(): hub_table = lax.all_gather(hub_local, ('hub', 'rep'), axis=0, tiled=True)  14.8 us
    all_to_all x1, starting transfers between devices, on_device(): lax.all_to_all(outgoing, 'blk', split_axis=0, concat_axis=0, tiled=True)  13.1 us
    gather x1, local copies, waits for them, and re-layouts, on_device(): outgoing = local_proj[picked]  8.98 us
    all_to_all x1, waiting for transfers between devices, sent_and_summed(): pieces = lax.all_to_all(in_blocks(array, dim, size), axis, 0, 0, tiled=True)  5.33 us
    dot_general x1, matrix products, on_device(): neigh_sum = jnp.dot(select, gathered, preferred_element_type=jnp.float32)  2.95 us
  transfers between devices with their start and end apart: 2, of which 2 were waited for; matrix products, arithmetic and copies ran while one was open for 9% of the time, Pallas kernels for 0%

commit v1 on v0

v1 whole, which is shorter than its diff:
```python
import jax
import jax.numpy as jnp
from jax import lax
from jax.sharding import PartitionSpec as P

NZ, NX = 16, 4


def one_hot(ids, count):
    return (ids[None, :] == jnp.arange(count, dtype=jnp.int32)[:, None]).astype(jnp.bfloat16)


def dot(a, b, dims):
    return lax.dot_general(a, b, dims, preferred_element_type=jnp.float32)


def on_device(
    source_feats,
    target_feats,
    hub_feats,
    weight_self,
    weight_neigh,
    bias_vector,
    send_rows,
    edge_target,
    edge_slot,
    hub_source,
    hub_target,
):
    width = weight_neigh.shape[1]
    rows = source_feats.shape[0]
    cap = send_rows.shape[2]
    targets = target_feats.shape[0]
    group = lax.axis_size(("hub", "rep"))
    mine = hub_feats.shape[0]
    hubs = group * mine
    nz, nx = NZ, NX
    z_groups = [[z * nx + x for z in range(nz)] for x in range(nx)]
    x_groups = [[z * nx + x for x in range(nx)] for z in range(nz)]
    z = lax.axis_index("blk") // nx

    proj = jnp.dot(source_feats, weight_neigh, preferred_element_type=jnp.float32).astype(jnp.bfloat16)
    picked = send_rows[0].reshape(-1, width).astype(jnp.bfloat16)
    payload = jnp.concatenate([proj, picked], axis=0)
    column = lax.all_gather(payload, "blk", axis=0, tiled=False, axis_index_groups=z_groups)

    hub_local = jnp.dot(hub_feats, weight_neigh, preferred_element_type=jnp.float32).astype(jnp.bfloat16)
    hub_rows = dot(one_hot(hub_source[0], rows), proj, (((0,), (0,)), ((), ()))).astype(jnp.bfloat16)
    hub_select = one_hot(hub_target[0], hubs)
    hub_partial = dot(hub_select, hub_rows, (((1,), (0,)), ((), ())))
    hub_edges = jnp.sum(hub_select.astype(jnp.float32), axis=1)
    parts = jnp.concatenate(
        [
            hub_partial.reshape(group, mine, width),
            jnp.broadcast_to(hub_local.astype(jnp.float32)[None], (group, mine, width)),
            jnp.pad(hub_edges.reshape(group, 1, mine), ((0, 0), (0, 7), (0, width - mine))),
        ],
        axis=1,
    )
    got = lax.all_to_all(parts, ("hub", "rep"), 0, 0, tiled=True)
    hub_sum = jnp.sum(got[:, :mine], axis=0)
    hub_table = got[:, mine : 2 * mine].reshape(hubs, width).astype(jnp.bfloat16)
    hub_degree = jnp.sum(got[:, 2 * mine, :mine], axis=0)

    slots = nz * nx * cap + hubs
    select_t = one_hot(edge_target[0], targets)
    counts = dot(select_t, one_hot(edge_slot[0], slots), (((1,), (1,)), ((), ())))
    high = jnp.floor(counts * (1.0 / 256.0))
    low = (counts - 256.0 * high).astype(jnp.bfloat16)
    high = high.astype(jnp.bfloat16)
    degree = jnp.sum(select_t.astype(jnp.float32), axis=1)
    own = jnp.dot(target_feats, weight_self, preferred_element_type=jnp.float32)

    ids = column[:, rows:, :].reshape(nz, nz, nx * cap)
    ids = lax.dynamic_index_in_dim(ids, z, 1, keepdims=False)
    pick = (
        ids[:, :, None] == jnp.arange(rows, dtype=jnp.int32)[None, None, :].astype(jnp.bfloat16)
    ).astype(jnp.bfloat16)
    blocks = dot(pick, column[:, :rows, :], (((2,), (1,)), ((0,), (0,)))).astype(jnp.bfloat16)
    outgoing = blocks.reshape(nz, nx, cap, width).transpose(1, 0, 2, 3)
    arrived = lax.all_to_all(outgoing, "blk", 0, 0, tiled=True, axis_index_groups=x_groups)
    arrived = arrived.transpose(1, 0, 2, 3).reshape(nz * nx * cap, width)
    table = jnp.concatenate([arrived, hub_table], axis=0)
    neigh_sum = jnp.dot(low, table, preferred_element_type=jnp.float32) + 256.0 * jnp.dot(
        high, table, preferred_element_type=jnp.float32
    )
    vertex_out = jnp.maximum(
        own + neigh_sum / jnp.maximum(degree, 1.0)[:, None] + bias_vector[None, :], 0.0
    ).astype(jnp.bfloat16)
    own_hub = jnp.dot(hub_feats, weight_self, preferred_element_type=jnp.float32)
    hub_out = jnp.maximum(
        own_hub + hub_sum / jnp.maximum(hub_degree, 1.0)[:, None] + bias_vector[None, :], 0.0
    ).astype(jnp.bfloat16)
    return (vertex_out, hub_out)


def solution(mesh):
    rows2 = P(("blk", "hub", "rep"), None)
    in_specs = (
        rows2, rows2, rows2, P(), P(), P(),
        P(("blk", "hub", "rep"), None, None),
        rows2, rows2, rows2, rows2,
    )
    return jax.shard_map(
        on_device, mesh=mesh, in_specs=in_specs, out_specs=(rows2, rows2), check_vma=False
    )
```

time: 129 us -> 128 us (level)
  the two profiles are of different devices: /device:TPU:1 before, /device:TPU:32 now
where the time goes in v1:
time: 128 us; the launch traced here: 127 us
  waiting for transfers between devices  57.5 us (45%)
  matrix products  28.3 us (22%)
  starting transfers between devices  20.4 us (16%)
  between operations  14.2 us (11%)
  other arithmetic  4.12 us (3%)
  local copies, waits for them, and re-layouts  2.68 us (2%)
    all_gather x1, waiting for transfers between devices, on_device(): lax.all_gather(payload, 'blk', axis=0, tiled=False, axis_index_groups=z_g...  47.5 us
    dot_general x3, matrix products, dot(): return lax.dot_general(a, b, dims, preferred_element_type=jnp.float32)  20 us
    all_to_all x1, starting transfers between devices, on_device(): got = lax.all_to_all(parts, ('hub', 'rep'), 0, 0, tiled=True)  16.2 us
    all_to_all x1, waiting for transfers between devices, on_device(): lax.all_to_all(outgoing, 'blk', 0, 0, tiled=True, axis_index_groups=x_gro...  10 us
    all_to_all x1, starting transfers between devices, on_device(): lax.all_to_all(outgoing, 'blk', 0, 0, tiled=True, axis_index_groups=x_gro...  4.22 us
    dot_general x1, matrix products, on_device(): jnp.dot(low, table, preferred_element_type=jnp.float32)  3.37 us
  transfers between devices with their start and end apart: 3, of which 2 were waited for; matrix products, arithmetic and copies ran while one was open for 21% of the time, Pallas kernels for 0%

profile of v1, /device:TPU:32, one launch (start us, length us, event | category | flops | bytes accessed | tf_op | source)
XLA Modules:
  0.0 127.3 jit_solution(2170834041840909265)
XLA Ops:
  7.2 0.0 copy-start
  7.2 0.0 all-gather.3.cloned.1.call-start
  7.2 0.8 convert_element_type.64
  8.0 0.1 copy.23
  8.1 0.1 convert_element_type.65
  8.2 0.0 copy-start.4
  8.2 0.0 copy-start.5
  8.2 1.3 %convolution_convert_fusion.1 = bf16[256,256]{1,0:T(8,128)(2,1)S(1)} fusion(bf16[256,512]{1,0:T(8,128)(2,1)} %param.11, bf16[512,256]{1,0:T(8,128)(2,1)} %param.15), kind=kOutput, calls=%fused_computation.28 | convolution fusion | flops 67174400 | bytes 655360 | tf_op jit(solution)/shard_map/dot_general | solution.py:42
  9.5 0.7 pad_maximum_fusion.3
  10.1 0.0 all-gather.3.cloned.1.call-update
  10.2 0.8 convert_reduce_fusion.1
  11.0 0.1 reshape.41
  11.1 1.1 fusion.32
  12.2 1.2 fusion.28
  13.4 0.9 select_maximum_fusion
  14.3 16.2 %all-to-all-start.1 = ((f32[16,40,256]{2,1,0:T(8,128)}), f32[16,40,256]{2,1,0:T(8,128)S(1)}, u32[]{:S(2)}, u32[]{:S(2)}) async-start(f32[16,40,256]{2,1,0:T(8,128)} %select_maximum_fusion), calls=%async_computation.1 | async-start | bytes 1310720 | tf_op jit(solution)/shard_map/all_to_all | solution.py:60
  30.5 0.0 copy-done.4
  30.5 0.0 copy-done.5
  30.5 16.7 %fusion = f32[512,2304]{1,0:T(8,128)} fusion(s32[4096]{0:T(1024)S(1)} %bitcast.37, s32[4096]{0:T(1024)S(1)} %bitcast.38), kind=kOutput, calls=%fused_computation.1 | convolution fusion | flops 9675210752 | bytes 4751360 | tf_op jit(solution)/shard_map/dot_general | solution.py:14
  47.2 0.9 convert_reduce_fusion
  48.1 47.5 %all-gather.3.cloned.1.call-done = bf16[4224,256]{1,0:T(8,128)(2,1)} async-done(((bf16[264,256]{1,0:T(8,128)(2,1)}), bf16[4224,256]{1,0:T(8,128)(2,1)}) %all-gather.3.cloned.1.call-update) | async-done | bytes 2162704 | tf_op jit(solution)/shard_map/all_gather | solution.py:45
  95.6 0.8 slice.21
  96.5 2.1 %fusion.14 = bf16[16,128,256]{2,1,0:T(8,128)(2,1)S(1)} fusion(bf16[16,264,256]{2,1,0:T(8,128)(2,1)} %bitcast.36, bf16[256]{0:T(256)(128)(2,1)S(1)} %iota_convert_fusion, bf16[16,128]{1,0:T(8,128)(2,1)S(1)} %bitcast.32), kind=kOutput, calls=%fused_computation.18 | convolution fusion | flops 269484032 | bytes 3150336 | tf_op jit(solution)/shard_map/dot_general | solution.py:14
  98.6 0.0 copy-start.1
  98.6 0.0 copy-start.2
  98.6 0.0 copy-start.3
  98.7 1.1 copy.30
  99.8 0.0 all-to-all-done.1
  99.8 4.2 %all-to-all-start = ((bf16[4,16,32,256]{3,2,1,0:T(8,128)(2,1)}), bf16[4,16,32,256]{3,2,1,0:T(8,128)(2,1)S(1)}, u32[]{:S(2)}, u32[]{:S(2)}) async-start(bf16[4,16,32,256]{3,2,1,0:T(8,128)(2,1)} %bitcast.24), calls=%async_computation | async-start | bytes 2097152 | tf_op jit(solution)/shard_map/all_to_all | solution.py:81
  104.1 0.0 copy-done.1
  104.1 0.0 copy-done.2
  104.1 0.0 copy-done.3
  104.1 0.8 fusion.31
  104.9 10.0 %all-to-all-done = bf16[4,16,32,256]{3,2,1,0:T(8,128)(2,1)S(1)} async-done(((bf16[4,16,32,256]{3,2,1,0:T(8,128)(2,1)}), bf16[4,16,32,256]{3,2,1,0:T(8,128)(2,1)S(1)}, u32[]{:S(2)}, u32[]{:S(2)}) %all-to-all-start) | async-done | bytes 1048608 | tf_op jit(solution)/shard_map/all_to_all | solution.py:81
  114.9 0.0 slice-start
  114.9 0.1 copy.26
  115.0 0.0 slice-start.1
  115.0 3.4 %fusion.7 = f32[512,256]{1,0:T(8,128)S(1)} fusion(f32[512,2304]{1,0:T(8,128)} %fusion, bf16[256,256]{1,0:T(8,128)(2,1)S(1)} %bitcast.30, bf16[2048,256]{1,0:T(8,128)(2,1)S(1)} %bitcast.26), kind=kOutput, calls=%fused_computation.11 | convolution fusion | flops 612237312 | bytes 6422528 | tf_op jit(solution)/shard_map/dot_general | solution.py:84
  118.4 0.1 slice-done
  118.5 0.1 slice-done.1
  118.6 0.8 fusion.33
  119.4 0.0 copy-done
  119.4 1.0 fusion.27
  (11 shorter events, 0.2 us)
Async XLA Ops:
  7.2 112.2 %copy-start = (bf16[512,512]{1,0:T(8,128)(2,1)S(1)}, bf16[512,512]{1,0:T(8,128)(2,1)}, u32[]{:S(2)}) copy-start(bf16[512,512]{1,0:T(8,128)(2,1)} %param.12) | copy-start | bytes 1572868
  7.2 88.4 %all-gather.3.cloned.1.call-start = ((), (), s32[]{:S(2)}) async-start(), calls=%async_computation.2 | async-start | bytes 2297856 | tf_op jit(solution)/shard_map/all_gather | solution.py:45
  8.2 22.3 %copy-start.4 = (s32[1,4096]{1,0:T(1,128)S(1)}, s32[1,4096]{1,0:T(1,128)}, u32[]{:S(2)}) copy-start(s32[1,4096]{1,0:T(1,128)} %param.19) | copy-start | bytes 49156
  8.2 22.3 %copy-start.5 = (s32[1,4096]{1,0:T(1,128)S(1)}, s32[1,4096]{1,0:T(1,128)}, u32[]{:S(2)}) copy-start(s32[1,4096]{1,0:T(1,128)} %param.18) | copy-start | bytes 49156
  14.3 85.4 %all-to-all-start.1 = ((f32[16,40,256]{2,1,0:T(8,128)}), f32[16,40,256]{2,1,0:T(8,128)S(1)}, u32[]{:S(2)}, u32[]{:S(2)}) async-start(f32[16,40,256]{2,1,0:T(8,128)} %select_maximum_fusion), calls=%async_computation.1 | async-start | bytes 1310720 | tf_op jit(solution)/shard_map/all_to_all | solution.py:60
  98.6 5.4 %copy-start.1 = (bf16[512,256]{1,0:T(8,128)(2,1)S(1)}, bf16[512,256]{1,0:T(8,128)(2,1)}, u32[]{:S(2)}) copy-start(bf16[512,256]{1,0:T(8,128)(2,1)} %param.14) | copy-start | bytes 786436
  98.6 5.4 %copy-start.2 = (bf16[16,512]{1,0:T(8,128)(2,1)S(1)}, bf16[16,512]{1,0:T(8,128)(2,1)}, u32[]{:S(2)}) copy-start(bf16[16,512]{1,0:T(8,128)(2,1)} %param.13) | copy-start | bytes 49156
  98.6 5.4 %copy-start.3 = (f32[256]{0:T(256)S(1)}, f32[256]{0:T(256)}, u32[]{:S(2)}) copy-start(f32[256]{0:T(256)} %param.16) | copy-start | bytes 3076
  99.8 15.1 %all-to-all-start = ((bf16[4,16,32,256]{3,2,1,0:T(8,128)(2,1)}), bf16[4,16,32,256]{3,2,1,0:T(8,128)(2,1)S(1)}, u32[]{:S(2)}, u32[]{:S(2)}) async-start(bf16[4,16,32,256]{3,2,1,0:T(8,128)(2,1)} %bitcast.24), calls=%async_computation | async-start | bytes 2097152 | tf_op jit(solution)/shard_map/all_to_all | solution.py:81
  114.9 3.6 %slice-start = ((s8[4718592]{0:T(1024)(128)(4,1)}), s8[4194304]{0:T(1024)(128)(4,1)S(1)}, s32[]{:S(2)}) async-start(s8[4718592]{0:T(1024)(128)(4,1)} %bitcast.41), calls=%async_computation.3 | async-start | bytes 8388608
  115.0 3.6 %slice-start.1 = ((s8[4718592]{0:T(1024)(128)(4,1)}), s8[524288]{0:T(1024)(128)(4,1)S(1)}, s32[]{:S(2)}) async-start(s8[4718592]{0:T(1024)(128)(4,1)} %bitcast.41), calls=%async_computation.4 | async-start | bytes 1048576
Sparse Core Ops, SparseCore 0:
  11.2 84.3 all-gather.2

commit v2 on v1

v2 whole, which is shorter than its diff:
```python
import functools

import jax
import jax.numpy as jnp
from jax import lax
from jax.experimental import pallas as pl
from jax.experimental.pallas import tpu as pltpu
from jax.sharding import PartitionSpec as P

MESH = pl.DeviceIdType.MESH
NZ, NX = 16, 4
CHUNKS = 4
LANES = 128
BF, F32 = jnp.bfloat16, jnp.float32


def dot(a, b, contract):
    return lax.dot_general(a, b, ((contract[:1], contract[1:]), ((), ())), preferred_element_type=F32)


def one_hot(ids, first, count):
    rows = lax.broadcasted_iota(jnp.int32, (count, ids.shape[1]), 0)
    return jnp.where(rows == ids - first, 1.0, 0.0).astype(BF)


def kernel(
    ny, nr,
    src, tgt, hubf, ws, wn, bias, picks, et, es, hs, ht,
    vout, hout,
    col, idb, xbuf, table, hubp, hubr, tsel, cnt, cacc, dacc, acc, own,
    ring_s, ring_r, ids_s, ids_r, x_s, x_r, tab_s, tab_r, part_s, part_r,
):
    nz, nx, group = NZ, NX, ny * nr
    rows, width = col.shape[1], col.shape[2]
    cap = picks.shape[1]
    block = nx * cap
    mine = hubf.shape[0]
    hubs = group * mine
    base = nz * block
    chunk = rows // CHUNKS
    half = nz // 2
    edges = et.shape[1]
    part = edges // 2
    pair = 2 * LANES

    blk = lax.axis_index("blk")
    z, x = lax.div(blk, nx), lax.rem(blk, nx)
    m = lax.axis_index("hub") * nr + lax.axis_index("rep")

    def at_z(step):
        return lax.rem(z + step + nz, nz)

    def to_x(dx):
        return {"blk": z * nx + lax.rem(x + dx, nx)}

    def to_member(k):
        other = lax.rem(m + k, group)
        return {"hub": lax.div(other, nr), "rep": lax.rem(other, nr)}

    def ring_next(way):
        return {"blk": at_z(1 if way == 0 else -1) * nx + x}

    def remote(a, b, s, r, device):
        return pltpu.make_async_remote_copy(
            src_ref=a, dst_ref=b, send_sem=s, recv_sem=r, device_id=device, device_id_type=MESH
        )

    def ring_copy(way, owner, step, c):
        at = col.at[owner, pl.ds(c * chunk, chunk), :]
        return remote(at, at, ring_s.at[way, step - 1, c], ring_r.at[way, step - 1, c], ring_next(way))

    def ids_copy(way, owner, step):
        at = idb.at[owner]
        return remote(at, at, ids_s.at[way, step - 1], ids_r.at[way, step - 1], ring_next(way))

    def x_copy(owner, dx):
        there = lax.rem(x + dx, nx)
        a = xbuf.at[owner, pl.ds(pl.multiple_of(there * cap, cap), cap), :]
        b = table.at[pl.ds(pl.multiple_of((owner * nx + x) * cap, cap), cap), :]
        return remote(a, b, x_s.at[dx - 1, owner], x_r.at[dx - 1, owner], to_x(dx))

    def tab_copy(k):
        at = table.at[pl.ds(pl.multiple_of(base + m * mine, mine), mine), :]
        return remote(at, at, tab_s.at[k - 1], tab_r.at[k - 1], to_member(k))

    def part_copy(k):
        other = lax.rem(m + k, group)
        a = hubp.at[pl.ds(pl.multiple_of(other * mine, mine), mine), :]
        return remote(a, hubr.at[m], part_s.at[k - 1], part_r.at[k - 1], to_member(k))

    barrier = pltpu.get_barrier_semaphore()
    for way in (0, 1):
        pl.semaphore_signal(barrier, inc=1, device_id=ring_next(way), device_id_type=MESH)
    for dx in range(1, nx):
        pl.semaphore_signal(barrier, inc=1, device_id=to_x(dx), device_id_type=MESH)
    for k in range(1, group):
        pl.semaphore_signal(barrier, inc=1, device_id=to_member(k), device_id_type=MESH)

    col[z] = dot(src[...], wn[...], (1, 0)).astype(BF)
    table[pl.ds(pl.multiple_of(base + m * mine, mine), mine), :] = dot(hubf[...], wn[...], (1, 0)).astype(BF)
    ids = [picks[pl.ds(j, nz, stride=nx), :] for j in range(nx)]
    idb[z] = jnp.concatenate(ids, axis=1).astype(F32).astype(BF)

    pl.semaphore_wait(barrier, 2 + (nx - 1) + (group - 1))

    for way in (0, 1):
        ids_copy(way, z, 1).start()
    for c in range(CHUNKS):
        for way in (0, 1):
            ring_copy(way, z, 1, c).start()
    for k in range(1, group):
        tab_copy(k).start()

    def choose(owner):
        tile = idb[owner].astype(F32)
        which = lax.broadcasted_iota(jnp.int32, tile.shape, 0)
        row = jnp.sum(jnp.where(which == z, tile, 0.0), axis=0, keepdims=True)
        pick = one_hot(row.astype(jnp.int32), 0, rows)
        xbuf[owner] = dot(pick, col[owner], (0, 0)).astype(BF)
        keep = xbuf[owner, pl.ds(pl.multiple_of(x * cap, cap), cap), :]
        table[pl.ds(pl.multiple_of((owner * nx + x) * cap, cap), cap), :] = keep

    def hand_out(owner):
        for dx in range(1, nx):
            x_copy(owner, dx).start()

    def count_half(n, h):
        marks = one_hot(es[:, h * part : (h + 1) * part], n * pair, pair)
        got = dot(tsel[:, h * part : (h + 1) * part], marks, (1, 1))
        if h == 0:
            cacc[...] = got
            return
        got = got + cacc[...]
        dacc[...] += got[:, :LANES] + got[:, LANES:]
        high = jnp.floor(got * (1.0 / 256.0))
        low = got - 256.0 * high
        for j in range(2):
            lanes = slice(j * LANES, (j + 1) * LANES)
            cnt[2 * n + j, :, :LANES] = low[:, lanes].astype(BF)
            cnt[2 * n + j, :, LANES:] = high[:, lanes].astype(BF)

    def add_slab(slab):
        start = slab * LANES if isinstance(slab, int) else pl.multiple_of(slab * LANES, LANES)
        t = table[pl.ds(start, LANES), :]
        both = jnp.concatenate([t, (t.astype(F32) * 256.0).astype(BF)], axis=0)
        acc[...] += dot(cnt[slab], both, (1, 0))

    def take(owner):
        for dx in range(1, nx):
            x_copy(owner, dx).wait_recv()
        add_slab(owner)

    def pass_on(step, c):
        for way in (0, 1):
            owner = at_z(-step if way == 0 else step)
            if c == 0:
                ids_copy(way, owner, step).wait_recv()
                ids_copy(way, owner, step + 1).start()
            ring_copy(way, owner, step, c).wait_recv()
            ring_copy(way, owner, step + 1, c).start()

    hub_rows = dot(one_hot(hs[...], 0, rows), col[z], (0, 0)).astype(BF)
    marks = one_hot(ht[...], 0, hubs)
    hubp[:, :width] = dot(marks, hub_rows, (1, 0))
    hubp[:, width:] = jnp.broadcast_to(
        jnp.sum(marks.astype(F32), axis=1, keepdims=True), (hubs, LANES)
    )
    choose(z)
    tsel[...] = one_hot(et[...], 0, tgt.shape[0])
    acc[...] = jnp.zeros_like(acc)
    dacc[...] = jnp.zeros_like(dacc)
    for k in range(1, group):
        part_copy(k).start()
    hand_out(z)
    count_half(nz // 2, 0)
    count_half(nz // 2, 1)

    def early(step, carry):
        for c in range(CHUNKS):
            pass_on(step, c)
            if c == CHUNKS - 1:
                choose(at_z(-step))
                choose(at_z(step))
            count_half(2 * (step - 1) + c // 2, c % 2)
        hand_out(at_z(-step))
        hand_out(at_z(step))
        return carry

    lax.fori_loop(1, half // 2 + 1, early, 0)

    def late(step, carry):
        for c in range(CHUNKS):
            pass_on(step, c)
            if c == CHUNKS - 1:
                choose(at_z(-step))
                choose(at_z(step))
            back = 2 * (step - half // 2 - 1) + 1 + c // 2
            take(at_z(-back if c % 2 == 0 else back))
        hand_out(at_z(-step))
        hand_out(at_z(step))
        return carry

    lax.fori_loop(half // 2 + 1, half - 1, late, 0)

    step = half - 1
    for c in range(CHUNKS):
        for way in (0, 1):
            owner = at_z(-step if way == 0 else step)
            if c == 0:
                ids_copy(way, owner, step).wait_recv()
                if way == 0:
                    ids_copy(way, owner, half).start()
            ring_copy(way, owner, step, c).wait_recv()
            if way == c // (CHUNKS // 2):
                ring_copy(way, owner, half, c).start()
        if c == 0:
            own[...] = dot(tgt[...], ws[...], (1, 0)) + bias[...]
        if c == 1:
            take(z)
        if c == 2:
            for k in range(1, group):
                tab_copy(k).wait_recv()
            add_slab(nz)
            add_slab(nz + 1)
    choose(at_z(-step))
    choose(at_z(step))
    for k in range(1, group):
        part_copy(k).wait_recv()
    total = hubp[pl.ds(pl.multiple_of(m * mine, mine), mine), :]
    for k in range(1, group):
        total = total + hubr[lax.rem(m + k, group)]
    fed = total[:, :width] / jnp.maximum(total[:, width : width + 1], 1.0)
    mean = dot(hubf[...], ws[...], (1, 0)) + fed + bias[...]
    hout[...] = jnp.maximum(mean, 0.0).astype(hout.dtype)
    hand_out(at_z(-step))
    hand_out(at_z(step))
    take(at_z(-(half - 3)))
    take(at_z(half - 3))

    far = at_z(half)
    ids_copy(0, far, half).wait_recv()
    for c in range(CHUNKS):
        ring_copy(c // (CHUNKS // 2), far, half, c).wait_recv()
    choose(far)
    take(at_z(-(half - 2)))
    hand_out(far)
    take(at_z(half - 2))
    take(at_z(-step))
    take(at_z(step))
    scale = 1.0 / jnp.maximum(jnp.sum(dacc[...], axis=1, keepdims=True), 1.0)
    take(far)
    vout[...] = jnp.maximum(own[...] + acc[...] * scale, 0.0).astype(vout.dtype)

    def sent(step, carry):
        for way in (0, 1):
            ids_copy(way, z, step).wait_send()
            for c in range(CHUNKS):
                ring_copy(way, z, step, c).wait_send()
        return carry

    lax.fori_loop(1, half, sent, 0)
    ids_copy(0, z, half).wait_send()
    for c in range(CHUNKS):
        ring_copy(c // (CHUNKS // 2), z, half, c).wait_send()

    def sent_x(owner, carry):
        for dx in range(1, nx):
            x_copy(owner, dx).wait_send()
        return carry

    lax.fori_loop(0, nz, sent_x, 0)
    for k in range(1, group):
        tab_copy(k).wait_send()
        part_copy(k).wait_send()


def on_device(
    source_feats,
    target_feats,
    hub_feats,
    weight_self,
    weight_neigh,
    bias_vector,
    send_rows,
    edge_target,
    edge_slot,
    hub_source,
    hub_target,
):
    ny, nr = lax.axis_size("hub"), lax.axis_size("rep")
    rows, width = source_feats.shape[0], weight_neigh.shape[1]
    targets, mine, cap = target_feats.shape[0], hub_feats.shape[0], send_rows.shape[2]
    group = ny * nr
    hubs = group * mine
    slots = NZ * NX * cap + hubs
    edges = edge_target.shape[1]
    half = NZ // 2
    dma = pltpu.SemaphoreType.DMA
    vmem = pl.BlockSpec(memory_space=pltpu.VMEM)
    return pl.pallas_call(
        functools.partial(kernel, ny, nr),
        out_shape=(
            jax.ShapeDtypeStruct((targets, width), BF),
            jax.ShapeDtypeStruct((mine, width), BF),
        ),
        in_specs=[vmem] * 11,
        out_specs=(vmem, vmem),
        scratch_shapes=[
            pltpu.VMEM((NZ, rows, width), BF),
            pltpu.VMEM((NZ, NZ, NX * cap), BF),
            pltpu.VMEM((NZ, NX * cap, width), BF),
            pltpu.VMEM((slots, width), BF),
            pltpu.VMEM((hubs, width + LANES), F32),
            pltpu.VMEM((group, mine, width + LANES), F32),
            pltpu.VMEM((targets, edges), BF),
            pltpu.VMEM((slots // LANES, targets, 2 * LANES), BF),
            pltpu.VMEM((targets, 2 * LANES), F32),
            pltpu.VMEM((targets, LANES), F32),
            pltpu.VMEM((targets, width), F32),
            pltpu.VMEM((targets, width), F32),
            dma((2, half, CHUNKS)),
            dma((2, half, CHUNKS)),
            dma((2, half)),
            dma((2, half)),
            dma((NX - 1, NZ)),
            dma((NX - 1, NZ)),
            dma((group - 1,)),
            dma((group - 1,)),
            dma((group - 1,)),
            dma((group - 1,)),
        ],
        compiler_params=pltpu.CompilerParams(
            collective_id=0, has_side_effects=True, vmem_limit_bytes=40 * 1024 * 1024
        ),
    )(
        source_feats,
        target_feats,
        hub_feats,
        weight_self,
        weight_neigh,
        bias_vector.reshape(1, width),
        send_rows[0],
        edge_target,
        edge_slot,
        hub_source,
        hub_target,
    )


def solution(mesh):
    rows = P(("blk", "hub", "rep"), None)
    in_specs = (
        rows, rows, rows, P(), P(), P(),
        P(("blk", "hub", "rep"), None, None),
        rows, rows, rows, rows,
    )
    return jax.shard_map(
        on_device, mesh=mesh, in_specs=in_specs, out_specs=(rows, rows), check_vma=False
    )
```

time: 128 us -> 74.2 us (0.58)
  the two profiles are of different devices: /device:TPU:32 before, /device:TPU:1 now
where the time goes in v2:
time: 74.2 us; the launch traced here: 73 us
  Pallas kernels  64.9 us (87%)
  local copies, waits for them, and re-layouts  7.35 us (10%)
    pallas_call x1, Pallas kernels, on_device(): pl.pallas_call(functools.partial(kernel, ny, nr), out_shape=(jax.ShapeDty...  64.9 us
    unnamed x23, local copies, waits for them, and re-layouts  7.35 us

profile of v2, /device:TPU:1, one launch (start us, length us, event | category | flops | bytes accessed | tf_op | source)
XLA Modules:
  0.0 73.0 jit_solution(1158443333944053006)
XLA Ops:
  0.6 0.0 copy-start.7
  0.6 0.0 copy-start.4
  0.7 0.0 copy-start.5
  0.7 0.0 copy-start.6
  0.7 0.8 %copy.13 = s32[1,64,32]{2,1,0:T(8,128)S(1)} copy(s32[1,64,32]{1,2,0:T(8,128)} %param.17) | data formatting | bytes 16384 | tf_op args[6]
  1.5 0.0 copy-start.9
  1.5 0.0 copy-done.7
  1.5 0.0 copy-done.4
  1.5 0.0 copy-done.5
  1.5 0.0 copy-done.6
  1.5 0.6 copy-done.9
  2.2 0.0 copy-start
  2.2 1.0 %copy-done = bf16[512,512]{1,0:T(8,128)(2,1)S(1)} copy-done((bf16[512,512]{1,0:T(8,128)(2,1)S(1)}, bf16[512,512]{1,0:T(8,128)(2,1)}, u32[]{:S(2)}) %copy-start) | copy-done | bytes 524312
  3.2 0.0 copy-start.1
  3.2 0.9 %copy-done.1 = bf16[256,512]{1,0:T(8,128)(2,1)S(1)} copy-done((bf16[256,512]{1,0:T(8,128)(2,1)S(1)}, bf16[256,512]{1,0:T(8,128)(2,1)}, u32[]{:S(2)}) %copy-start.1) | copy-done | bytes 262168
  4.2 0.0 copy-start.2
  4.2 0.9 %copy-done.2 = bf16[512,256]{1,0:T(8,128)(2,1)S(1)} copy-done((bf16[512,256]{1,0:T(8,128)(2,1)S(1)}, bf16[512,256]{1,0:T(8,128)(2,1)}, u32[]{:S(2)}) %copy-start.2) | copy-done | bytes 262168
  5.1 0.0 copy-start.3
  5.1 0.9 %copy-done.3 = bf16[512,256]{1,0:T(8,128)(2,1)S(1)} copy-done((bf16[512,256]{1,0:T(8,128)(2,1)S(1)}, bf16[512,256]{1,0:T(8,128)(2,1)}, u32[]{:S(2)}) %copy-start.3) | copy-done | bytes 262168
  6.1 0.0 copy-start.8
  6.1 0.7 copy-done.8
  6.8 64.9 %shard_map.122 = (bf16[512,256]{1,0:T(8,128)(2,1)S(1)}, bf16[16,256]{1,0:T(8,128)(2,1)S(1)}) custom-call(bf16[256,512]{1,0:T(8,128)(2,1)S(1)} %copy-done.1, bf16[512,512]{1,0:T(8,128)(2,1)S(1)} %copy-done, bf16[16,512]{1,0:T(8,128)(2,1)S(1)} %copy-done.4, bf16[512,256]{1,0:T(8,128)(2,1)S(1)} %copy-done.2, bf16[512,256]{1,0:T(8,128)(2,1)S(1)} %copy-done.3, ...), custom_call_target="tpu_custom_call" | custom-call | tf_op jit(solution)/shard_map/pallas_call | solution.py:300
  71.7 0.7 copy.16
  72.4 0.6 copy.17
Async XLA Ops:
  0.6 0.9 %copy-start.7 = (s32[1,512]{1,0:T(1,128)S(1)}, s32[1,512]{1,0:T(1,128)}, u32[]{:S(2)}) copy-start(s32[1,512]{1,0:T(1,128)} %hs.1) | copy-start | bytes 6148
  0.6 0.9 %copy-start.4 = (bf16[16,512]{1,0:T(8,128)(2,1)S(1)}, bf16[16,512]{1,0:T(8,128)(2,1)}, u32[]{:S(2)}) copy-start(bf16[16,512]{1,0:T(8,128)(2,1)} %hubf.1) | copy-start | bytes 49156
  0.7 0.9 %copy-start.5 = (s32[1,4096]{1,0:T(1,128)S(1)}, s32[1,4096]{1,0:T(1,128)}, u32[]{:S(2)}) copy-start(s32[1,4096]{1,0:T(1,128)} %et.1) | copy-start | bytes 49156
  0.7 0.9 %copy-start.6 = (s32[1,4096]{1,0:T(1,128)S(1)}, s32[1,4096]{1,0:T(1,128)}, u32[]{:S(2)}) copy-start(s32[1,4096]{1,0:T(1,128)} %es.1) | copy-start | bytes 49156
  1.5 0.7 copy-start.9
  2.2 1.0 %copy-start = (bf16[512,512]{1,0:T(8,128)(2,1)S(1)}, bf16[512,512]{1,0:T(8,128)(2,1)}, u32[]{:S(2)}) copy-start(bf16[512,512]{1,0:T(8,128)(2,1)} %tgt.1) | copy-start | bytes 1572868
  3.2 0.9 %copy-start.1 = (bf16[256,512]{1,0:T(8,128)(2,1)S(1)}, bf16[256,512]{1,0:T(8,128)(2,1)}, u32[]{:S(2)}) copy-start(bf16[256,512]{1,0:T(8,128)(2,1)} %src.1) | copy-start | bytes 786436
  4.2 0.9 %copy-start.2 = (bf16[512,256]{1,0:T(8,128)(2,1)S(1)}, bf16[512,256]{1,0:T(8,128)(2,1)}, u32[]{:S(2)}) copy-start(bf16[512,256]{1,0:T(8,128)(2,1)} %ws.1) | copy-start | bytes 786436
  5.1 0.9 %copy-start.3 = (bf16[512,256]{1,0:T(8,128)(2,1)S(1)}, bf16[512,256]{1,0:T(8,128)(2,1)}, u32[]{:S(2)}) copy-start(bf16[512,256]{1,0:T(8,128)(2,1)} %wn.1) | copy-start | bytes 786436
  6.1 0.7 copy-start.8

commit v3 on v2

--- a/solution.py
+++ b/solution.py
@@ -10,8 +10,9 @@
 MESH = pl.DeviceIdType.MESH
 NZ, NX = 16, 4
 CHUNKS = 4
+RING = 5
 LANES = 128
-BF, F32 = jnp.bfloat16, jnp.float32
+BF, F32, F8 = jnp.bfloat16, jnp.float32, jnp.float8_e4m3fn
 
 
 def dot(a, b, contract):
@@ -19,20 +20,28 @@
 
 
 def one_hot(ids, first, count):
-    rows = lax.broadcasted_iota(jnp.int32, (count, ids.shape[1]), 0)
-    return jnp.where(rows == ids - first, 1.0, 0.0).astype(BF)
+    n = ids.shape[1]
+    parts = []
+    rows = lax.broadcasted_iota(jnp.int32, (256, LANES), 0).astype(F32).astype(BF)
+    rows = jnp.concatenate([rows] * (n // LANES), axis=1)
+    for at in range(0, count, 256):
+        near = jnp.broadcast_to(ids - (first + at), (16, n)).astype(F32).astype(BF)
+        near = jnp.concatenate([near] * 16, axis=0)
+        parts.append(jnp.where(rows == near, BF(1.0), BF(0.0)))
+    return parts[0] if len(parts) == 1 else jnp.concatenate(parts, axis=0)
 
 
 def kernel(
     ny, nr,
-    src, tgt, hubf, ws, wn, bias, picks, et, es, hs, ht,
+    src_h, wn_h, hubf_h, picks_h, hs_h, ht_h, et_h, es_h, tgt_h, ws_h, bias_h,
     vout, hout,
-    col, idb, xbuf, table, hubp, hubr, tsel, cnt, cacc, dacc, acc, own,
-    ring_s, ring_r, ids_s, ids_r, x_s, x_r, tab_s, tab_r, part_s, part_r,
+    src, wn, hubf, picks, hs, ht, et, es, tgt, ws, bias, turned,
+    col, idb, xbuf, table, hubp, hubr, tsel, cnt, cacc, dacc, acc, own, far_buf,
+    ring_s, ring_r, ids_s, ids_r, x_s, x_r, tab_s, tab_r, part_s, part_r, far_s, far_r, in_s,
 ):
     nz, nx, group = NZ, NX, ny * nr
     rows, width = col.shape[1], col.shape[2]
-    cap = picks.shape[1]
+    cap = picks.shape[0]
     block = nx * cap
     mine = hubf.shape[0]
     hubs = group * mine
@@ -73,6 +82,18 @@
         at = idb.at[owner]
         return remote(at, at, ids_s.at[way, step - 1], ids_r.at[way, step - 1], ring_next(way))
 
+    def far_copy(way, k, owner):
+        at = k - RING - 1
+        first, last = (0, block) if k < half else (way * block // 2, (way + 1) * block // 2)
+        there = at_z(k - RING if way == 0 else RING - k)
+        return remote(
+            far_buf.at[way, at, pl.ds(first, last - first), :],
+            xbuf.at[owner, pl.ds(first, last - first), :],
+            far_s.at[way, at],
+            far_r.at[way, at],
+            {"blk": there * nx + x},
+        )
+
     def x_copy(owner, dx):
         there = lax.rem(x + dx, nx)
         a = xbuf.at[owner, pl.ds(pl.multiple_of(there * cap, cap), cap), :]
@@ -88,44 +109,63 @@
         a = hubp.at[pl.ds(pl.multiple_of(other * mine, mine), mine), :]
         return remote(a, hubr.at[m], part_s.at[k - 1], part_r.at[k - 1], to_member(k))
 
+    inputs = (
+        (src_h, src), (wn_h, wn), (hubf_h, hubf), (picks_h, picks), (hs_h, hs), (ht_h, ht),
+        (et_h, et), (es_h, es), (tgt_h, tgt), (ws_h, ws), (bias_h, bias),
+    )
+    loads = [pltpu.make_async_copy(a, b, in_s.at[i]) for i, (a, b) in enumerate(inputs)]
+    for load in loads:
+        load.start()
+
     barrier = pltpu.get_barrier_semaphore()
-    for way in (0, 1):
-        pl.semaphore_signal(barrier, inc=1, device_id=ring_next(way), device_id_type=MESH)
+    reach = half - RING
+    for k in range(1, reach + 1):
+        for there in (at_z(k), at_z(-k)):
+            pl.semaphore_signal(barrier, inc=1, device_id={"blk": there * nx + x}, device_id_type=MESH)
     for dx in range(1, nx):
         pl.semaphore_signal(barrier, inc=1, device_id=to_x(dx), device_id_type=MESH)
     for k in range(1, group):
         pl.semaphore_signal(barrier, inc=1, device_id=to_member(k), device_id_type=MESH)
 
+    for load in loads[:4]:
+        load.wait()
     col[z] = dot(src[...], wn[...], (1, 0)).astype(BF)
     table[pl.ds(pl.multiple_of(base + m * mine, mine), mine), :] = dot(hubf[...], wn[...], (1, 0)).astype(BF)
-    ids = [picks[pl.ds(j, nz, stride=nx), :] for j in range(nx)]
-    idb[z] = jnp.concatenate(ids, axis=1).astype(F32).astype(BF)
-
-    pl.semaphore_wait(barrier, 2 + (nx - 1) + (group - 1))
-
+    turned[...] = picks[...].astype(F32).T
+    ids = [turned[pl.ds(j, nz, stride=nx), :] for j in range(nx)]
+    idb[z] = jnp.concatenate(ids, axis=1).astype(BF)
+
+    pl.semaphore_wait(barrier, 2 * reach + (nx - 1) + (group - 1))
+
+    for c in range(CHUNKS):
+        for way in (0, 1):
+            ring_copy(way, z, 1, c).start()
     for way in (0, 1):
         ids_copy(way, z, 1).start()
-    for c in range(CHUNKS):
-        for way in (0, 1):
-            ring_copy(way, z, 1, c).start()
     for k in range(1, group):
         tab_copy(k).start()
 
-    def choose(owner):
+    def chosen(owner, place):
         tile = idb[owner].astype(F32)
         which = lax.broadcasted_iota(jnp.int32, tile.shape, 0)
-        row = jnp.sum(jnp.where(which == z, tile, 0.0), axis=0, keepdims=True)
+        row = jnp.sum(jnp.where(which == place, tile, 0.0), axis=0, keepdims=True)
         pick = one_hot(row.astype(jnp.int32), 0, rows)
-        xbuf[owner] = dot(pick, col[owner], (0, 0)).astype(BF)
-        keep = xbuf[owner, pl.ds(pl.multiple_of(x * cap, cap), cap), :]
-        table[pl.ds(pl.multiple_of((owner * nx + x) * cap, cap), cap), :] = keep
+        return dot(pick, col[owner], (0, 0)).astype(BF)
+
+    def keep(owner):
+        mine_too = xbuf[owner, pl.ds(pl.multiple_of(x * cap, cap), cap), :]
+        table[pl.ds(pl.multiple_of((owner * nx + x) * cap, cap), cap), :] = mine_too
+
+    def choose(owner):
+        xbuf[owner] = chosen(owner, z)
+        keep(owner)
 
     def hand_out(owner):
         for dx in range(1, nx):
             x_copy(owner, dx).start()
 
     def count_half(n, h):
-        marks = one_hot(es[:, h * part : (h + 1) * part], n * pair, pair)
+        marks = one_hot(es[:, h * part : (h + 1) * part], n * pair, pair).astype(F8)
         got = dot(tsel[:, h * part : (h + 1) * part], marks, (1, 1))
         if h == 0:
             cacc[...] = got
@@ -153,12 +193,14 @@
     def pass_on(step, c):
         for way in (0, 1):
             owner = at_z(-step if way == 0 else step)
-            if c == 0:
+            ring_copy(way, owner, step, c).wait_recv()
+            ring_copy(way, owner, step + 1, c).start()
+            if c == CHUNKS - 1:
                 ids_copy(way, owner, step).wait_recv()
                 ids_copy(way, owner, step + 1).start()
-            ring_copy(way, owner, step, c).wait_recv()
-            ring_copy(way, owner, step + 1, c).start()
-
+
+    for load in loads[4:]:
+        load.wait()
     hub_rows = dot(one_hot(hs[...], 0, rows), col[z], (0, 0)).astype(BF)
     marks = one_hot(ht[...], 0, hubs)
     hubp[:, :width] = dot(marks, hub_rows, (1, 0))
@@ -166,7 +208,7 @@
         jnp.sum(marks.astype(F32), axis=1, keepdims=True), (hubs, LANES)
     )
     choose(z)
-    tsel[...] = one_hot(et[...], 0, tgt.shape[0])
+    tsel[...] = one_hot(et[...], 0, tgt.shape[0]).astype(F8)
     acc[...] = jnp.zeros_like(acc)
     dacc[...] = jnp.zeros_like(dacc)
     for k in range(1, group):
@@ -188,65 +230,61 @@
 
     lax.fori_loop(1, half // 2 + 1, early, 0)
 
-    def late(step, carry):
-        for c in range(CHUNKS):
-            pass_on(step, c)
+    for c in range(CHUNKS):
+        for way in (0, 1):
+            owner = at_z(-RING if way == 0 else RING)
+            ring_copy(way, owner, RING, c).wait_recv()
             if c == CHUNKS - 1:
-                choose(at_z(-step))
-                choose(at_z(step))
-            back = 2 * (step - half // 2 - 1) + 1 + c // 2
-            take(at_z(-back if c % 2 == 0 else back))
-        hand_out(at_z(-step))
-        hand_out(at_z(step))
-        return carry
-
-    lax.fori_loop(half // 2 + 1, half - 1, late, 0)
-
-    step = half - 1
-    for c in range(CHUNKS):
-        for way in (0, 1):
-            owner = at_z(-step if way == 0 else step)
-            if c == 0:
-                ids_copy(way, owner, step).wait_recv()
-                if way == 0:
-                    ids_copy(way, owner, half).start()
-            ring_copy(way, owner, step, c).wait_recv()
-            if way == c // (CHUNKS // 2):
-                ring_copy(way, owner, half, c).start()
+                ids_copy(way, owner, RING).wait_recv()
         if c == 0:
             own[...] = dot(tgt[...], ws[...], (1, 0)) + bias[...]
         if c == 1:
-            take(z)
-        if c == 2:
             for k in range(1, group):
                 tab_copy(k).wait_recv()
             add_slab(nz)
             add_slab(nz + 1)
-    choose(at_z(-step))
-    choose(at_z(step))
+            take(z)
+        if c == 2:
+            for back in (1, 2):
+                take(at_z(-back))
+                take(at_z(back))
+    beyond = range(half, RING, -1)
+    for k in beyond:
+        for way in (0, 1):
+            owner = at_z(-RING if way == 0 else RING)
+            far_buf[way, k - RING - 1] = chosen(owner, at_z(k - RING if way == 0 else RING - k))
+    for k in beyond:
+        for way in (0, 1):
+            far_copy(way, k, at_z(-RING if way == 0 else RING)).start()
+    choose(at_z(-RING))
+    choose(at_z(RING))
     for k in range(1, group):
         part_copy(k).wait_recv()
     total = hubp[pl.ds(pl.multiple_of(m * mine, mine), mine), :]
     for k in range(1, group):
         total = total + hubr[lax.rem(m + k, group)]
+    hand_out(at_z(-RING))
+    hand_out(at_z(RING))
     fed = total[:, :width] / jnp.maximum(total[:, width : width + 1], 1.0)
     mean = dot(hubf[...], ws[...], (1, 0)) + fed + bias[...]
     hout[...] = jnp.maximum(mean, 0.0).astype(hout.dtype)
-    hand_out(at_z(-step))
-    hand_out(at_z(step))
-    take(at_z(-(half - 3)))
-    take(at_z(half - 3))
-
+    for back in range(3, RING):
+        take(at_z(-back))
+        take(at_z(back))
+
+    for k in range(RING + 1, half + 1):
+        for way in (0, 1):
+            owner = at_z(-k if way == 0 else k)
+            far_copy(way, k, owner).wait_recv()
+            if k < half:
+                hand_out(owner)
+                keep(owner)
+    hand_out(at_z(half))
+    keep(at_z(half))
+    for back in range(RING, half):
+        take(at_z(-back))
+        take(at_z(back))
     far = at_z(half)
-    ids_copy(0, far, half).wait_recv()
-    for c in range(CHUNKS):
-        ring_copy(c // (CHUNKS // 2), far, half, c).wait_recv()
-    choose(far)
-    take(at_z(-(half - 2)))
-    hand_out(far)
-    take(at_z(half - 2))
-    take(at_z(-step))
-    take(at_z(step))
     scale = 1.0 / jnp.maximum(jnp.sum(dacc[...], axis=1, keepdims=True), 1.0)
     take(far)
     vout[...] = jnp.maximum(own[...] + acc[...] * scale, 0.0).astype(vout.dtype)
@@ -258,10 +296,10 @@
                 ring_copy(way, z, step, c).wait_send()
         return carry
 
-    lax.fori_loop(1, half, sent, 0)
-    ids_copy(0, z, half).wait_send()
-    for c in range(CHUNKS):
-        ring_copy(c // (CHUNKS // 2), z, half, c).wait_send()
+    lax.fori_loop(1, RING + 1, sent, 0)
+    for k in beyond:
+        for way in (0, 1):
+            far_copy(way, k, z).wait_send()
 
     def sent_x(owner, carry):
         for dx in range(1, nx):
@@ -295,6 +333,19 @@
     slots = NZ * NX * cap + hubs
     edges = edge_target.shape[1]
     half = NZ // 2
+    operands = (
+        source_feats,
+        weight_neigh,
+        hub_feats,
+        send_rows[0].T,
+        hub_source,
+        hub_target,
+        edge_target,
+        edge_slot,
+        target_feats,
+        weight_self,
+        bias_vector.reshape(1, width),
+    )
     dma = pltpu.SemaphoreType.DMA
     vmem = pl.BlockSpec(memory_space=pltpu.VMEM)
     return pl.pallas_call(
@@ -303,48 +354,42 @@
             jax.ShapeDtypeStruct((targets, width), BF),
             jax.ShapeDtypeStruct((mine, width), BF),
         ),
-        in_specs=[vmem] * 11,
+        in_specs=[pl.BlockSpec(memory_space=pltpu.HBM)] * 11,
         out_specs=(vmem, vmem),
-        scratch_shapes=[
+        scratch_shapes=[pltpu.VMEM(a.shape, a.dtype) for a in operands]
+        + [
+            pltpu.VMEM((NZ * NX, cap), F32),
             pltpu.VMEM((NZ, rows, width), BF),
             pltpu.VMEM((NZ, NZ, NX * cap), BF),
             pltpu.VMEM((NZ, NX * cap, width), BF),
             pltpu.VMEM((slots, width), BF),
             pltpu.VMEM((hubs, width + LANES), F32),
             pltpu.VMEM((group, mine, width + LANES), F32),
-            pltpu.VMEM((targets, edges), BF),
+            pltpu.VMEM((targets, edges), F8),
             pltpu.VMEM((slots // LANES, targets, 2 * LANES), BF),
             pltpu.VMEM((targets, 2 * LANES), F32),
             pltpu.VMEM((targets, LANES), F32),
             pltpu.VMEM((targets, width), F32),
             pltpu.VMEM((targets, width), F32),
-            dma((2, half, CHUNKS)),
-            dma((2, half, CHUNKS)),
-            dma((2, half)),
-            dma((2, half)),
+            pltpu.VMEM((2, half - RING, NX * cap, width), BF),
+            dma((2, RING, CHUNKS)),
+            dma((2, RING, CHUNKS)),
+            dma((2, RING)),
+            dma((2, RING)),
             dma((NX - 1, NZ)),
             dma((NX - 1, NZ)),
             dma((group - 1,)),
             dma((group - 1,)),
             dma((group - 1,)),
             dma((group - 1,)),
+            dma((2, half - RING)),
+            dma((2, half - RING)),
+            dma((len(operands),)),
         ],
         compiler_params=pltpu.CompilerParams(
-            collective_id=0, has_side_effects=True, vmem_limit_bytes=40 * 1024 * 1024
+            collective_id=0, has_side_effects=True, vmem_limit_bytes=67043328
         ),
-    )(
-        source_feats,
-        target_feats,
-        hub_feats,
-        weight_self,
-        weight_neigh,
-        bias_vector.reshape(1, width),
-        send_rows[0],
-        edge_target,
-        edge_slot,
-        hub_source,
-        hub_target,
-    )
+    )(*operands)
 
 
 def solution(mesh):

time: 74.2 us -> 61.1 us (0.82)
  the two profiles are of different devices: /device:TPU:1 before, /device:TPU:64 now
where the time goes in v3:
time: 61.1 us; the launch traced here: 60.9 us
  Pallas kernels  57.9 us (95%)
  local copies, waits for them, and re-layouts  2.28 us (4%)
  between operations  0.65 us (1%)
    pallas_call x1, Pallas kernels, on_device(): pl.pallas_call(functools.partial(kernel, ny, nr), out_shape=(jax.ShapeDty...  57.9 us
    unnamed x4, local copies, waits for them, and re-layouts  2.28 us

profile of v3, /device:TPU:64, one launch (start us, length us, event | category | flops | bytes accessed | tf_op | source)
XLA Modules:
  0.0 60.9 jit_solution(16266091564834207467)
XLA Ops:
  0.6 57.9 %shard_map.122 = (bf16[512,256]{1,0:T(8,128)(2,1)}, bf16[16,256]{1,0:T(8,128)(2,1)}) custom-call(bf16[256,512]{1,0:T(8,128)(2,1)} %src_h.1, bf16[512,256]{1,0:T(8,128)(2,1)} %wn_h.1, bf16[16,512]{1,0:T(8,128)(2,1)} %hubf_h.1, s32[32,64]{1,0:T(8,128)} %bitcast.4, s32[1,512]{1,0:T(1,128)} %hs_h.1, s32[1,512]{1,0:T(1,128)} %ht_h.1, s32[1,4096]{1,0:T(1,128)} %et_h.1, ...), custom_call_target="tpu_custom_call" | custom-call | tf_op jit(solution)/shard_map/pallas_call | solution.py:351
  58.6 0.0 copy-start
  58.6 1.7 %copy.15 = bf16[512,256]{1,0:T(8,128)(2,1)} copy(bf16[512,256]{1,0:T(8,128)(2,1)} %get-tuple-element.4) | data formatting | bytes 524288
  60.3 0.0 copy-done
  60.3 0.6 copy.16
Async XLA Ops:
  58.6 1.7 %copy-start = (bf16[16,256]{1,0:T(8,128)(2,1)S(1)}, bf16[16,256]{1,0:T(8,128)(2,1)}, u32[]{:S(2)}) copy-start(bf16[16,256]{1,0:T(8,128)(2,1)} %get-tuple-element.5) | copy-start | bytes 24580

commit v4 on v3

--- a/solution.py
+++ b/solution.py
@@ -10,8 +10,9 @@
 MESH = pl.DeviceIdType.MESH
 NZ, NX = 16, 4
 CHUNKS = 4
-RING = 5
+RING = 6
 LANES = 128
+DIRECT = (7, 8)
 BF, F32, F8 = jnp.bfloat16, jnp.float32, jnp.float8_e4m3fn
 
 
@@ -37,7 +38,7 @@
     vout, hout,
     src, wn, hubf, picks, hs, ht, et, es, tgt, ws, bias, turned,
     col, idb, xbuf, table, hubp, hubr, tsel, cnt, cacc, dacc, acc, own, far_buf,
-    ring_s, ring_r, ids_s, ids_r, x_s, x_r, tab_s, tab_r, part_s, part_r, far_s, far_r, in_s,
+    ring_s, ring_r, ids_s, ids_r, x_s, x_r, tab_s, tab_r, part_s, part_r, far_s, far_r, end_s, end_r, in_s,
 ):
     nz, nx, group = NZ, NX, ny * nr
     rows, width = col.shape[1], col.shape[2]
@@ -94,6 +95,24 @@
             {"blk": there * nx + x},
         )
 
+    def end_places(way, k):
+        return range(nx) if k < half else range(way * nx // 2, (way + 1) * nx // 2)
+
+    def end_copy(way, k, owner, sender, place):
+        at = k - RING - 1
+        there = lax.rem(z + nz + (k - RING) - 2 * (k - RING) * way, nz)
+        return remote(
+            far_buf.at[way, at, pl.ds(place * cap, cap), :],
+            table.at[pl.ds(pl.multiple_of((owner * nx + sender) * cap, cap), cap), :],
+            end_s.at[way, at, place],
+            end_r.at[way, at, sender],
+            {"blk": there * nx + place},
+        )
+
+    def end_wait(way, k, owner):
+        for sender in range(nx):
+            end_copy(way, k, owner, sender, 0).wait_recv()
+
     def x_copy(owner, dx):
         there = lax.rem(x + dx, nx)
         a = xbuf.at[owner, pl.ds(pl.multiple_of(there * cap, cap), cap), :]
@@ -119,9 +138,15 @@
 
     barrier = pltpu.get_barrier_semaphore()
     reach = half - RING
-    for k in range(1, reach + 1):
-        for there in (at_z(k), at_z(-k)):
-            pl.semaphore_signal(barrier, inc=1, device_id={"blk": there * nx + x}, device_id_type=MESH)
+    near = [(there, j) for k in range(1, reach + 1) if RING + k in DIRECT and k < reach
+            for there in (at_z(k), at_z(-k)) for j in range(nx)]
+    near += [(there, x) for k in range(1, reach + 1) if RING + k not in DIRECT for there in (at_z(k), at_z(-k))]
+    if RING > 1 and RING + 1 in DIRECT and reach == 1:
+        near += [(at_z(1), x), (at_z(-1), x)]
+    if half in DIRECT:
+        near += [(lax.rem(z + nz - reach + 2 * reach * lax.div(x, nx // 2), nz), j) for j in range(nx)]
+    for there, j in near:
+        pl.semaphore_signal(barrier, inc=1, device_id={"blk": there * nx + j}, device_id_type=MESH)
     for dx in range(1, nx):
         pl.semaphore_signal(barrier, inc=1, device_id=to_x(dx), device_id_type=MESH)
     for k in range(1, group):
@@ -135,7 +160,7 @@
     ids = [turned[pl.ds(j, nz, stride=nx), :] for j in range(nx)]
     idb[z] = jnp.concatenate(ids, axis=1).astype(BF)
 
-    pl.semaphore_wait(barrier, 2 * reach + (nx - 1) + (group - 1))
+    pl.semaphore_wait(barrier, len(near) + (nx - 1) + (group - 1))
 
     for c in range(CHUNKS):
         for way in (0, 1):
@@ -230,6 +255,15 @@
 
     lax.fori_loop(1, half // 2 + 1, early, 0)
 
+    for step in range(half // 2 + 1, RING):
+        for c in range(CHUNKS):
+            pass_on(step, c)
+        choose(at_z(-step))
+        choose(at_z(step))
+        take(z)
+        hand_out(at_z(-step))
+        hand_out(at_z(step))
+
     for c in range(CHUNKS):
         for way in (0, 1):
             owner = at_z(-RING if way == 0 else RING)
@@ -243,7 +277,6 @@
                 tab_copy(k).wait_recv()
             add_slab(nz)
             add_slab(nz + 1)
-            take(z)
         if c == 2:
             for back in (1, 2):
                 take(at_z(-back))
@@ -255,7 +288,12 @@
             far_buf[way, k - RING - 1] = chosen(owner, at_z(k - RING if way == 0 else RING - k))
     for k in beyond:
         for way in (0, 1):
-            far_copy(way, k, at_z(-RING if way == 0 else RING)).start()
+            owner = at_z(-RING if way == 0 else RING)
+            if k not in DIRECT:
+                far_copy(way, k, owner).start()
+                continue
+            for place in end_places(way, k):
+                end_copy(way, k, owner, x, place).start()
     choose(at_z(-RING))
     choose(at_z(RING))
     for k in range(1, group):
@@ -275,18 +313,29 @@
     for k in range(RING + 1, half + 1):
         for way in (0, 1):
             owner = at_z(-k if way == 0 else k)
+            if k in DIRECT:
+                continue
             far_copy(way, k, owner).wait_recv()
-            if k < half:
+            if k < half or way == 1:
                 hand_out(owner)
                 keep(owner)
-    hand_out(at_z(half))
-    keep(at_z(half))
-    for back in range(RING, half):
-        take(at_z(-back))
-        take(at_z(back))
+    take(at_z(-RING))
+    take(at_z(RING))
+    for k in sorted(range(RING + 1, half), key=lambda k: (k in DIRECT, k)):
+        for way in (0, 1):
+            owner = at_z(-k if way == 0 else k)
+            if k in DIRECT:
+                end_wait(way, k, owner)
+                add_slab(owner)
+            else:
+                take(owner)
     far = at_z(half)
     scale = 1.0 / jnp.maximum(jnp.sum(dacc[...], axis=1, keepdims=True), 1.0)
-    take(far)
+    if half in DIRECT:
+        end_wait(lax.div(x, nx // 2), half, far)
+        add_slab(far)
+    else:
+        take(far)
     vout[...] = jnp.maximum(own[...] + acc[...] * scale, 0.0).astype(vout.dtype)
 
     def sent(step, carry):
@@ -299,14 +348,20 @@
     lax.fori_loop(1, RING + 1, sent, 0)
     for k in beyond:
         for way in (0, 1):
-            far_copy(way, k, z).wait_send()
-
-    def sent_x(owner, carry):
+            if k not in DIRECT:
+                far_copy(way, k, z).wait_send()
+                continue
+            for place in end_places(way, k):
+                end_copy(way, k, z, x, place).wait_send()
+
+    def sent_x(step, carry):
+        owner = lax.rem(z + nz - handed + step, nz)
         for dx in range(1, nx):
             x_copy(owner, dx).wait_send()
         return carry
 
-    lax.fori_loop(0, nz, sent_x, 0)
+    handed = max(k for k in range(half + 1) if k not in DIRECT)
+    lax.fori_loop(0, handed + min(handed, half - 1) + 1, sent_x, 0)
     for k in range(1, group):
         tab_copy(k).wait_send()
         part_copy(k).wait_send()
@@ -384,6 +439,8 @@
             dma((group - 1,)),
             dma((2, half - RING)),
             dma((2, half - RING)),
+            dma((2, half - RING, NX)),
+            dma((2, half - RING, NX)),
             dma((len(operands),)),
         ],
         compiler_params=pltpu.CompilerParams(

time: 61.1 us -> 60 us (0.982)
  the two profiles are of different devices: /device:TPU:64 before, /device:TPU:2 now
where the time goes in v4:
time: 60 us; the launch traced here: 59.8 us
  Pallas kernels  56.9 us (95%)
  local copies, waits for them, and re-layouts  2.28 us (4%)
  between operations  0.65 us (1%)
    pallas_call x1, Pallas kernels, on_device(): pl.pallas_call(functools.partial(kernel, ny, nr), out_shape=(jax.ShapeDty...  56.9 us
    unnamed x4, local copies, waits for them, and re-layouts  2.28 us

profile of v4, /device:TPU:2, one launch (start us, length us, event | category | flops | bytes accessed | tf_op | source)
XLA Modules:
  0.0 59.8 jit_solution(14249090177163061690)
XLA Ops:
  0.6 56.9 %shard_map.122 = (bf16[512,256]{1,0:T(8,128)(2,1)}, bf16[16,256]{1,0:T(8,128)(2,1)}) custom-call(bf16[256,512]{1,0:T(8,128)(2,1)} %src_h.1, bf16[512,256]{1,0:T(8,128)(2,1)} %wn_h.1, bf16[16,512]{1,0:T(8,128)(2,1)} %hubf_h.1, s32[32,64]{1,0:T(8,128)} %bitcast.4, s32[1,512]{1,0:T(1,128)} %hs_h.1, s32[1,512]{1,0:T(1,128)} %ht_h.1, s32[1,4096]{1,0:T(1,128)} %et_h.1, ...), custom_call_target="tpu_custom_call" | custom-call | tf_op jit(solution)/shard_map/pallas_call | solution.py:406
  57.5 0.0 copy-start
  57.6 1.7 %copy.15 = bf16[512,256]{1,0:T(8,128)(2,1)} copy(bf16[512,256]{1,0:T(8,128)(2,1)} %get-tuple-element.4) | data formatting | bytes 524288
  59.2 0.0 copy-done
  59.2 0.6 %copy.16 = bf16[16,256]{1,0:T(8,128)(2,1)} copy(bf16[16,256]{1,0:T(8,128)(2,1)S(1)} %copy-done) | data formatting | bytes 16384
Async XLA Ops:
  57.5 1.7 %copy-start = (bf16[16,256]{1,0:T(8,128)(2,1)S(1)}, bf16[16,256]{1,0:T(8,128)(2,1)}, u32[]{:S(2)}) copy-start(bf16[16,256]{1,0:T(8,128)(2,1)} %get-tuple-element.5) | copy-start | bytes 24580
